TPU v7x, 32 devices: a whole 2x2x4 slice. The times are simulated.
32 devices in a mesh: ep: 8 (over z, x), tp: 4 (over y, core).
Axes of the slice: x: 2, y: 2, z: 4, core: 2. Of those that a mesh axis runs over, the one named last changes fastest.
Arguments:
- tokens: bfloat16 [1024, 4096], P('ep', 'tp'), may hold values from -6 to 6
- expert_ids: int32 [1024, 2], P('ep'), may hold values from 0 to 7, all different within a row; in each aligned block of 128 rows (0 to 127, 128 to 255, ...) at most 40 rows name the same one
- gates: float32 [1024, 2], P('ep'), may hold values from 0.1 to 1
- gate_weight: bfloat16 [4096, 57344], P('tp', 'ep'), may hold values from -0.09375 to 0.09375
- up_weight: bfloat16 [4096, 57344], P('tp', 'ep'), may hold values from -0.09375 to 0.09375
- down_weight: bfloat16 [57344, 4096], P('ep', 'tp'), may hold values from -0.0625 to 0.0625
Outputs:
- mixed: bfloat16 [1024, 4096], P('ep', 'tp')
- expert_counts: float32 [8], replicated
- aux_loss: float32 [], replicated
Inputs may be any that keep to these rules, and one draw needn't show every extreme that they name: `expert_ids`: each token names 2 different experts. Among the tokens of one index of ep no expert is named more than 40 times, and in every draw some expert is named exactly 40 times by some index's tokens; every expert is named somewhere.
All inputs are finite; a program needn't handle non-finite values.
Results may differ from a plain program's by a relative error of at most 0.008.
Values may be sent and summed in bfloat16 or wider, within the bound.
A program may use at most 128 MiB of HBM per device.

v0:
```python
import jax
import jax.numpy as jnp
from jax import lax
from jax.sharding import PartitionSpec as P

EXPERTS = 8
TOP = 2
CAP = 40


def expert_rows(received, gate_weight, up_weight, down_weight):
    width = gate_weight.shape[1]
    stacked = jnp.concatenate((gate_weight, up_weight), axis=1)
    summed = lax.psum_scatter(
        jnp.dot(received, stacked, preferred_element_type=jnp.float32),
        "tp",
        scatter_dimension=0,
        tiled=True,
    )
    gate_pre = summed[:, :width]
    up_pre = summed[:, width:]
    hidden = (jax.nn.silu(gate_pre) * up_pre).astype(jnp.bfloat16)
    return jnp.dot(
        lax.all_gather(hidden, "tp", axis=0, tiled=True),
        down_weight,
        preferred_element_type=jnp.float32,
    ).astype(jnp.bfloat16)


def per_device(tokens, expert_ids, gates, gate_weight, up_weight, down_weight):
    count_tok = tokens.shape[0]
    quarter = tokens.shape[1]
    replicas = lax.axis_size("ep") // EXPERTS
    slots_all = EXPERTS * CAP
    flat_ids = expert_ids.reshape(-1)
    onehot = (flat_ids[:, None] == jnp.arange(EXPERTS, dtype=jnp.int32)[None, :]).astype(jnp.int32)
    before = jnp.cumsum(onehot, axis=0) - onehot
    target = flat_ids * CAP + jnp.sum(before * onehot, axis=1)
    matches = (
        target.reshape(count_tok, TOP)[:, :, None]
        == jnp.arange(slots_all, dtype=jnp.int32)[None, None, :]
    ).astype(jnp.float32)
    combine = jnp.sum(matches * gates[:, :, None], axis=1)
    selector = jnp.sum(matches, axis=1).astype(jnp.bfloat16)
    dispatched = jnp.einsum(
        "ts,td->sd", selector, tokens, preferred_element_type=jnp.float32
    ).astype(jnp.bfloat16)
    copies = jnp.broadcast_to(
        dispatched.reshape(EXPERTS, 1, CAP, quarter), (EXPERTS, replicas, CAP, quarter)
    )
    received = lax.all_to_all(
        copies.reshape(-1, quarter), "ep", split_axis=0, concat_axis=0, tiled=True
    )
    partial_value = expert_rows(received, gate_weight, up_weight, down_weight)
    returned = lax.all_to_all(partial_value, "ep", split_axis=0, concat_axis=0, tiled=True)
    results = jnp.sum(returned.reshape(EXPERTS, replicas, CAP, quarter).astype(jnp.float32), axis=1)
    results = results.reshape(slots_all, quarter)
    mixed = jnp.dot(
        combine, results, precision=lax.Precision.HIGHEST, preferred_element_type=jnp.float32
    ).astype(jnp.bfloat16)
    counts = jnp.sum(onehot, axis=0).astype(jnp.float32)
    totals = jnp.sum(onehot.astype(jnp.float32) * gates.reshape(-1)[:, None], axis=0)
    counts, totals = lax.psum((counts, totals), "ep")
    tokens_all = count_tok * lax.axis_size("ep")
    aux_loss = EXPERTS * jnp.sum(counts / (TOP * tokens_all) * (totals / tokens_all))
    return (mixed, counts, aux_loss)


def solution(mesh):
    placed = (
        P("ep", "tp"),
        P("ep", None),
        P("ep", None),
        P("tp", "ep"),
        P("tp", "ep"),
        P("ep", "tp"),
    )
    return jax.shard_map(
        per_device, mesh=mesh, in_specs=placed, out_specs=(P("ep", "tp"), P(), P()), check_vma=False
    )
```

profile of v0, /device:TPU:0, one launch (start us, length us, event | category | flops | bytes accessed | tf_op | source)
XLA Modules:
  0.0 289.2 jit_solution(7241450728386867234)
XLA Ops:
  7.2 0.0 copy-start
  7.2 0.0 reduce-scatter.2.cloned.1.call-start
  7.2 0.8 copy.23
  8.0 0.1 eq.38
  8.2 0.1 eq.42
  8.3 0.6 reduce-window.6
  8.9 0.2 slice_reduce_fusion
  9.2 0.1 convert_reduce_fusion.1
  9.3 0.1 reduce_sum.61
  9.5 0.1 copy.25
  9.5 0.7 multiply_add_fusion
  10.2 0.8 convert_reduce_fusion
  11.0 0.0 copy-done
  11.0 0.3 convolution_convert_fusion.1
  11.3 24.7 %all_to_all.24 = bf16[8,40,1024]{2,1,0:T(8,128)(2,1)S(1)} all-to-all(bf16[8,40,1024]{2,1,0:T(8,128)(2,1)S(1)} %bitcast.16), channel_id=1, replica_groups=mesh['ep'=8,'tp'=4] {'ep'}, dimensions={0} | all-to-all | bytes 1310720 | tf_op jit(solution)/shard_map/all_to_all | solution.py:51
  36.1 24.3 %fusion = f32[320,14336]{1,0:T(8,128)} fusion(bf16[320,1024]{1,0:T(8,128)(2,1)S(1)} %bitcast.17, bf16[1024,7168]{1,0:T(8,128)(2,1)} %param.10, bf16[1024,7168]{1,0:T(8,128)(2,1)} %param.9), kind=kOutput, calls=%fused_computation | convolution fusion | flops 9453961216 | bytes 48365568 | tf_op jit(solution)/shard_map/dot_general | solution.py:15
  60.4 0.0 reduce-scatter.2.cloned.1.call-update
  60.4 0.0 all-gather.2.cloned.1.call-start
  60.5 133.4 %reduce-scatter.2.cloned.1.call-done = f32[80,14336]{1,0:T(8,128)} async-done(((f32[320,14336]{1,0:T(8,128)}), f32[80,14336]{1,0:T(8,128)}) %reduce-scatter.2.cloned.1.call-update) | async-done | bytes 4587536 | tf_op jit(solution)/shard_map/reduce_scatter | solution.py:14
  193.9 4.0 %fusion.4 = bf16[80,7168]{1,0:T(8,128)(2,1)} fusion(f32[80,14336]{1,0:T(8,128)} %reduce-scatter.2.cloned.1.call-done), kind=kLoop, calls=%fused_computation.5 | loop fusion | flops 3440640 | bytes 5734400 | tf_op jit(solution)/shard_map/convert_element_type | solution.py:22
  197.9 0.0 all-gather.2.cloned.1.call-update
  197.9 0.0 copy-start.2
  197.9 0.0 copy-start.1
  197.9 36.8 %all-gather.2.cloned.1.call-done = bf16[320,7168]{1,0:T(8,128)(2,1)} async-done(((bf16[80,7168]{1,0:T(8,128)(2,1)}), bf16[320,7168]{1,0:T(8,128)(2,1)}) %all-gather.2.cloned.1.call-update) | async-done | bytes 4587536 | tf_op jit(solution)/shard_map/all_gather | solution.py:24
  234.8 12.3 %convolution_convert_fusion = bf16[320,1024]{1,0:T(8,128)(2,1)} fusion(bf16[320,7168]{1,0:T(8,128)(2,1)} %all-gather.2.cloned.1.call-done, bf16[7168,1024]{1,0:T(8,128)(2,1)} %param.11), kind=kOutput, calls=%fused_computation.6 | convolution fusion | flops 4697948160 | bytes 19922944 | tf_op jit(solution)/shard_map/dot_general | solution.py:23
  247.1 5.5 %all-to-all-start.1 = ((bf16[8,40,1024]{2,1,0:T(8,128)(2,1)}), bf16[8,40,1024]{2,1,0:T(8,128)(2,1)S(1)}, u32[]{:S(2)}, u32[]{:S(2)}) async-start(bf16[8,40,1024]{2,1,0:T(8,128)(2,1)} %bitcast.4), calls=%async_computation.2 | async-start | bytes 1310720 | tf_op jit(solution)/shard_map/all_to_all | solution.py:55
  252.6 0.0 copy-done.2
  252.6 0.1 copy.26
  252.7 0.1 mul.46
  252.8 0.1 fusion.9
  253.0 25.6 %all-reduce = (f32[8]{0:T(128)S(1)}, f32[8]{0:T(128)S(1)}) all-reduce(f32[8]{0:T(128)S(1)} %convert_element_type.40, f32[8]{0:T(128)S(1)} %fusion.9), channel_id=1, replica_groups=mesh['ep'=8,'tp'=4] {'ep'}, use_global_device_ids=true, to_apply=%region_7.8 | all-reduce | flops 16 | bytes 128 | tf_op jit(solution)/shard_map/psum | solution.py:63
  278.6 0.0 copy-start.3
  278.6 0.6 multiply_reduce_fusion
  279.8 0.0 all-to-all-done.1
  279.8 1.3 convolution_convert_fusion.2
  281.2 0.0 copy-done.3
  281.2 0.0 copy-done.1
  (4 shorter events, 0.1 us)
Async XLA Ops:
  7.2 3.9 %copy-start = (bf16[128,1024]{1,0:T(8,128)(2,1)S(1)}, bf16[128,1024]{1,0:T(8,128)(2,1)}, u32[]{:S(2)}) copy-start(bf16[128,1024]{1,0:T(8,128)(2,1)} %param.6) | copy-start | bytes 786436
  7.2 186.7 %reduce-scatter.2.cloned.1.call-start = ((), (), s32[]{:S(2)}) async-start(), calls=%async_computation.3 | async-start | bytes 22937600 | tf_op jit(solution)/shard_map/reduce_scatter | solution.py:14
  60.4 174.3 %all-gather.2.cloned.1.call-start = ((), (), s32[]{:S(2)}) async-start(), calls=%async_computation.4 | async-start | bytes 5734400 | tf_op jit(solution)/shard_map/all_gather | solution.py:24
  197.9 54.7 %copy-start.2 = (f32[128,2]{0,1:T(2,128)S(1)}, f32[128,2]{0,1:T(2,128)}, u32[]{:S(2)}) copy-start(f32[128,2]{0,1:T(2,128)} %param.8) | copy-start | bytes 3076
  197.9 83.3 %copy-start.1 = (bf16[128,1024]{1,0:T(8,128)(2,1)S(1)}, bf16[128,1024]{1,0:T(8,128)(2,1)}, u32[]{:S(2)}) copy-start(bf16[128,1024]{1,0:T(8,128)(2,1)} %param.6) | copy-start | bytes 786436
  247.1 32.8 %all-to-all-start.1 = ((bf16[8,40,1024]{2,1,0:T(8,128)(2,1)}), bf16[8,40,1024]{2,1,0:T(8,128)(2,1)S(1)}, u32[]{:S(2)}, u32[]{:S(2)}) async-start(bf16[8,40,1024]{2,1,0:T(8,128)(2,1)} %bitcast.4), calls=%async_computation.2 | async-start | bytes 1310720 | tf_op jit(solution)/shard_map/all_to_all | solution.py:55
  278.6 2.6 copy-start.3
Sparse Core Ops, SparseCore 0:
  60.5 133.3 reduce-scatter.1
  198.0 36.6 all-gather.1
where the time goes:
time: 289 us
  waiting for transfers between devices  170 us (59%)
  blocking collectives  50.3 us (17%)
  matrix products  38.3 us (13%)
  between operations  15.9 us (6%)
  other arithmetic  6.94 us (2%)
  starting transfers between devices  5.59 us (2%)
    reduce_scatter x1, waiting for transfers between devices, expert_rows(): lax.psum_scatter(jnp.dot(received, stacked, preferred_element_type=jnp.fl...  133 us
    all_gather x1, waiting for transfers between devices, expert_rows(): lax.all_gather(hidden, 'tp', axis=0, tiled=True)  36.8 us
    psum x1, blocking collectives, per_device(): counts, totals = lax.psum((counts, totals), 'ep')  25.6 us
    all_to_all x1, blocking collectives, per_device(): lax.all_to_all(copies.reshape(-1, quarter), 'ep', split_axis=0, concat_ax...  24.7 us
    dot_general x1, matrix products, expert_rows(): jnp.dot(received, stacked, preferred_element_type=jnp.float32)  24.3 us
    dot_general x1, matrix products, expert_rows(): jnp.dot(lax.all_gather(hidden, 'tp', axis=0, tiled=True), down_weight, pr...  12.3 us
  transfers between devices with their start and end apart: 3, of which 2 were waited for; matrix products, arithmetic and copies ran while one was open for 0% of the time, Pallas kernels for 0%

commit v1 on v0

--- a/solution.py
+++ b/solution.py
@@ -1,30 +1,262 @@
+import functools
+
 import jax
 import jax.numpy as jnp
 from jax import lax
+from jax.experimental import pallas as pl
+from jax.experimental.pallas import tpu as pltpu
 from jax.sharding import PartitionSpec as P
 
 EXPERTS = 8
 TOP = 2
 CAP = 40
+MESH = pl.DeviceIdType.MESH
+RECV = 8
+LOCAL = 4
+WEIGHTS = 3
+
+
+def for_pieces(count, body):
+    piece = max(p for p in range(16, 321, 16) if count % p == 0)
+    if piece == count:
+        body(0, piece)
+        return
+
+    def step(i, carry):
+        body(pl.multiple_of(i * piece, piece), piece)
+        return carry
+
+    lax.fori_loop(0, count // piece, step, 0)
+
+
+def expert_kernel(
+    steps, chunk, x_ref, gate_hbm, up_hbm, down_hbm, out_ref,
+    gate_w, up_w, down_w, near_send, near_recv, keep, far_send, far_recv, own, hidden, total,
+    weight_sem, near_s, near_r, far_s, far_r, share_s, share_r, give_s, give_r, pass_s, pass_r,
+):
+    rows = x_ref.shape[0]
+    half = rows // 2
+    quarter = rows // 4
+    me = lax.axis_index("tp")
+    low = lax.rem(me, 2)
+    high = me // 2
+    near = high * 2 + (1 - low)
+    far = (1 - high) * 2 + low
+    keep_at = pl.multiple_of(low * half, half)
+    send_at = pl.multiple_of((1 - low) * half, half)
+    mine_in = pl.multiple_of(high * quarter, quarter)
+    other_in = pl.multiple_of((1 - high) * quarter, quarter)
+    mine = pl.multiple_of(low * half + high * quarter, quarter)
+    other = pl.multiple_of(low * half + (1 - high) * quarter, quarter)
+
+    barrier = pltpu.get_barrier_semaphore()
+    for peer in (near, far):
+        pl.semaphore_signal(barrier, inc=1, device_id={"tp": peer}, device_id_type=MESH)
+
+    def remote(src, dst, send, recv, peer):
+        return pltpu.make_async_remote_copy(
+            src_ref=src, dst_ref=dst, send_sem=send, recv_sem=recv,
+            device_id={"tp": peer}, device_id_type=MESH,
+        )
+
+    def columns(i):
+        return pl.ds(pl.multiple_of(i * chunk, chunk), chunk)
+
+    def load_gate(i):
+        s = lax.rem(i, WEIGHTS)
+        return pltpu.make_async_copy(gate_hbm.at[:, columns(i)], gate_w.at[s], weight_sem.at[0, s])
+
+    def load_up(i):
+        s = lax.rem(i, WEIGHTS)
+        return pltpu.make_async_copy(up_hbm.at[:, columns(i)], up_w.at[s], weight_sem.at[1, s])
+
+    def load_down(i):
+        s = lax.rem(i, WEIGHTS)
+        return pltpu.make_async_copy(down_hbm.at[columns(i), :], down_w.at[s], weight_sem.at[2, s])
+
+    def near_copy(i):
+        s, r = lax.rem(i, LOCAL), lax.rem(i, RECV)
+        return remote(near_send.at[s], near_recv.at[r], near_s.at[s], near_r.at[r], near)
+
+    def far_copy(i):
+        s, r = lax.rem(i, LOCAL), lax.rem(i, RECV)
+        return remote(far_send.at[s], far_recv.at[r], far_s.at[s], far_r.at[r], far)
+
+    def block(i, at):
+        return hidden.at[lax.rem(i, RECV), pl.ds(at, quarter), :]
+
+    def share_copy(i):
+        r = lax.rem(i, RECV)
+        return remote(block(i, mine), block(i, mine), share_s.at[r], share_r.at[r], far)
+
+    def give_copy(i):
+        r = lax.rem(i, RECV)
+        return remote(block(i, mine), block(i, mine), give_s.at[r], give_r.at[r], near)
+
+    def pass_copy(i):
+        r = lax.rem(i, RECV)
+        return remote(block(i, other), block(i, other), pass_s.at[r], pass_r.at[r], near)
+
+    for i in range(min(2, steps)):
+        load_gate(i).start()
+        load_up(i).start()
+
+    def clear(at, size):
+        total[pl.ds(at, size), :] = jnp.zeros((size, total.shape[1]), jnp.float32)
+
+    for_pieces(rows, clear)
+    pl.semaphore_wait(barrier, 2)
+
+    def iteration(i, carry):
+        @pl.when(i + 2 < steps)
+        def _():
+            load_gate(i + 2).start()
+            load_up(i + 2).start()
+
+        @pl.when((i >= 4) & (i - 4 < steps))
+        def _():
+            load_down(i - 4).start()
+
+        @pl.when(i < steps)
+        def _():
+            load_gate(i).wait()
+            load_up(i).wait()
+            s = lax.rem(i, LOCAL)
+            w = lax.rem(i, WEIGHTS)
+
+            def sent(at, size):
+                x = x_ref[pl.ds(send_at + at, size), :]
+                for k, weight in enumerate((gate_w, up_w)):
+                    near_send[s, pl.ds(at, size), k * chunk:(k + 1) * chunk] = jnp.dot(
+                        x, weight[w], preferred_element_type=jnp.float32
+                    ).astype(jnp.bfloat16)
+
+            for_pieces(half, sent)
+            near_copy(i).start()
+
+            def kept(at, size):
+                x = x_ref[pl.ds(keep_at + at, size), :]
+                for k, weight in enumerate((gate_w, up_w)):
+                    keep[s, pl.ds(at, size), k * chunk:(k + 1) * chunk] = jnp.dot(
+                        x, weight[w], preferred_element_type=jnp.float32
+                    )
+
+            for_pieces(half, kept)
+
+        @pl.when((i >= 1) & (i - 1 < steps))
+        def _():
+            j = i - 1
+            s, r = lax.rem(j, LOCAL), lax.rem(j, RECV)
+            near_copy(j).wait()
+
+            def summed(at, size):
+                far_send[s, pl.ds(at, size), :] = (
+                    keep[s, pl.ds(other_in + at, size), :]
+                    + near_recv[r, pl.ds(other_in + at, size), :].astype(jnp.float32)
+                ).astype(jnp.bfloat16)
+
+            for_pieces(quarter, summed)
+            far_copy(j).start()
+
+            def held(at, size):
+                own[s, pl.ds(at, size), :] = (
+                    keep[s, pl.ds(mine_in + at, size), :]
+                    + near_recv[r, pl.ds(mine_in + at, size), :].astype(jnp.float32)
+                )
+
+            for_pieces(quarter, held)
+
+        @pl.when((i >= 3) & (i - 3 < steps))
+        def _():
+            j = i - 3
+            s, r = lax.rem(j, LOCAL), lax.rem(j, RECV)
+            far_copy(j).wait()
+
+            def activate(at, size):
+                both = own[s, pl.ds(at, size), :] + far_recv[r, pl.ds(at, size), :].astype(jnp.float32)
+                gate_pre = both[:, :chunk]
+                up_pre = both[:, chunk:]
+                hidden[r, pl.ds(mine + at, size), :] = (
+                    gate_pre / (1.0 + jnp.exp(-gate_pre)) * up_pre
+                ).astype(jnp.bfloat16)
+
+            for_pieces(quarter, activate)
+            share_copy(j).start()
+            give_copy(j).start()
+
+        @pl.when((i >= 5) & (i - 5 < steps))
+        def _():
+            share_copy(i - 5).wait()
+            pass_copy(i - 5).start()
+
+        @pl.when((i >= 6) & (i - 6 < steps))
+        def _():
+            j = i - 6
+            r, w = lax.rem(j, RECV), lax.rem(j, WEIGHTS)
+            give_copy(j).wait()
+            pass_copy(j).wait()
+            load_down(j).wait()
+
+            def add(at, size):
+                total[pl.ds(at, size), :] += jnp.dot(
+                    hidden[r, pl.ds(at, size), :], down_w[w], preferred_element_type=jnp.float32
+                )
+
+            for_pieces(rows, add)
+
+        return carry
+
+    lax.fori_loop(0, steps + 6, iteration, 0)
+
+    def finish(at, size):
+        out_ref[pl.ds(at, size), :] = total[pl.ds(at, size), :].astype(jnp.bfloat16)
+
+    for_pieces(rows, finish)
 
 
 def expert_rows(received, gate_weight, up_weight, down_weight):
+    rows, depth = received.shape
     width = gate_weight.shape[1]
-    stacked = jnp.concatenate((gate_weight, up_weight), axis=1)
-    summed = lax.psum_scatter(
-        jnp.dot(received, stacked, preferred_element_type=jnp.float32),
-        "tp",
-        scatter_dimension=0,
-        tiled=True,
-    )
-    gate_pre = summed[:, :width]
-    up_pre = summed[:, width:]
-    hidden = (jax.nn.silu(gate_pre) * up_pre).astype(jnp.bfloat16)
-    return jnp.dot(
-        lax.all_gather(hidden, "tp", axis=0, tiled=True),
-        down_weight,
-        preferred_element_type=jnp.float32,
-    ).astype(jnp.bfloat16)
+    out = down_weight.shape[1]
+    chunk = 256 if width % 256 == 0 else 128
+    steps = width // chunk
+    half, quarter = rows // 2, rows // 4
+    vmem, hbm = pl.BlockSpec(memory_space=pltpu.VMEM), pl.BlockSpec(memory_space=pl.ANY)
+    dma = pltpu.SemaphoreType.DMA
+    bf16, f32 = jnp.bfloat16, jnp.float32
+    return pl.pallas_call(
+        functools.partial(expert_kernel, steps, chunk),
+        out_shape=jax.ShapeDtypeStruct((rows, out), bf16),
+        in_specs=[vmem, hbm, hbm, hbm],
+        out_specs=vmem,
+        scratch_shapes=[
+            pltpu.VMEM((WEIGHTS, depth, chunk), bf16),
+            pltpu.VMEM((WEIGHTS, depth, chunk), bf16),
+            pltpu.VMEM((WEIGHTS, chunk, out), bf16),
+            pltpu.VMEM((LOCAL, half, 2 * chunk), bf16),
+            pltpu.VMEM((RECV, half, 2 * chunk), bf16),
+            pltpu.VMEM((LOCAL, half, 2 * chunk), f32),
+            pltpu.VMEM((LOCAL, quarter, 2 * chunk), bf16),
+            pltpu.VMEM((RECV, quarter, 2 * chunk), bf16),
+            pltpu.VMEM((LOCAL, quarter, 2 * chunk), f32),
+            pltpu.VMEM((RECV, rows, chunk), bf16),
+            pltpu.VMEM((rows, out), f32),
+            dma((3, WEIGHTS)),
+            dma((LOCAL,)), dma((RECV,)),
+            dma((LOCAL,)), dma((RECV,)),
+            dma((RECV,)), dma((RECV,)),
+            dma((RECV,)), dma((RECV,)),
+            dma((RECV,)), dma((RECV,)),
+        ],
+        compiler_params=pltpu.CompilerParams(
+            collective_id=0, has_side_effects=True, vmem_limit_bytes=60 * 1024 * 1024
+        ),
+        cost_estimate=pl.CostEstimate(
+            flops=2 * rows * width * (2 * depth + out),
+            bytes_accessed=2 * width * (2 * depth + out),
+            transcendentals=0,
+        ),
+    )(received, gate_weight, up_weight, down_weight)
 
 
 def per_device(tokens, expert_ids, gates, gate_weight, up_weight, down_weight):

time: 289 us -> 148 us (0.51)
  waiting for transfers between devices: 170 us -> 0.01 us
  Pallas kernels: 0 us -> 83.6 us
  matrix products: 38.3 us -> 1.65 us
  between operations: 15.9 us -> 2.51 us
  other arithmetic: 6.94 us -> 2.96 us
    reduce_scatter x1 -> x0, waiting for transfers between devices: 133 us -> none  [expert_rows(): lax.psum_scatter(jnp.dot(received, stacked, preferred_element_type=jnp.fl...]
    pallas_call x0 -> x1, Pallas kernels: none -> 83.6 us  [expert_rows(): pl.pallas_call(functools.partial(expert_kernel, steps, chunk), out_shape=...]
    all_gather x1 -> x0, waiting for transfers between devices: 36.8 us -> none  [expert_rows(): lax.all_gather(hidden, 'tp', axis=0, tiled=True)]
    dot_general x2 -> x0, matrix products: 36.6 us -> none  [the longest x1 24.3 us: expert_rows(): jnp.dot(received, stacked, preferred_element_type=jnp.float32)]
    convert_element_type x1 -> x0, other arithmetic: 3.98 us -> none  [expert_rows(): hidden = (jax.nn.silu(gate_pre) * up_pre).astype(jnp.bfloat16)]
  transfers between devices with their start and end apart: 3 -> 1, of which waited for: 2 -> 0; matrix products, arithmetic and copies ran while one was open for 0% -> 1% of each run, Pallas kernels for 0% -> 0%
where the time goes in v1:
time: 148 us; the launch traced here: 147 us
  Pallas kernels  83.6 us (56%)
  blocking collectives  51.4 us (35%)
  starting transfers between devices  3.55 us (2%)
  other arithmetic  2.96 us (2%)
  between operations  2.51 us (2%)
  local copies, waits for them, and re-layouts  1.79 us (1%)
  matrix products  1.65 us (1%)
    pallas_call x1, Pallas kernels, expert_rows(): pl.pallas_call(functools.partial(expert_kernel, steps, chunk), out_shape=...  83.6 us
    psum x1, blocking collectives, per_device(): counts, totals = lax.psum((counts, totals), 'ep')  26.5 us
    all_to_all x1, blocking collectives, per_device(): lax.all_to_all(copies.reshape(-1, quarter), 'ep', split_axis=0, concat_ax...  24.9 us
    all_to_all x1, starting transfers between devices, per_device(): lax.all_to_all(partial_value, 'ep', split_axis=0, concat_axis=0, tiled=True)  3.55 us
  transfers between devices with their start and end apart: 1, of which 0 were waited for; matrix products, arithmetic and copies ran while one was open for 1% of the time, Pallas kernels for 0%

profile of v1, /device:TPU:0, one launch (start us, length us, event | category | flops | bytes accessed | tf_op | source)
XLA Modules:
  0.0 147.4 jit_solution(14796193533946906704)
XLA Ops:
  0.6 0.0 copy-start
  0.6 0.8 copy.23
  1.5 0.1 eq.38
  1.6 0.1 eq.42
  1.8 0.6 reduce-window.6
  2.4 0.2 slice_reduce_fusion
  2.6 0.1 convert_reduce_fusion.1
  2.8 0.1 reduce_sum.61
  2.9 0.1 copy.25
  3.0 0.7 multiply_add_fusion
  3.7 0.8 convert_reduce_fusion
  4.4 0.0 copy-done
  4.4 0.3 convolution_convert_fusion
  4.8 24.9 %all_to_all.23 = bf16[8,40,1024]{2,1,0:T(8,128)(2,1)} all-to-all(bf16[8,40,1024]{2,1,0:T(8,128)(2,1)S(1)} %bitcast.13), channel_id=1, replica_groups=mesh['ep'=8,'tp'=4] {'ep'}, dimensions={0} | all-to-all | bytes 1310720 | tf_op jit(solution)/shard_map/all_to_all | solution.py:283
  29.6 0.0 copy-start.1
  29.6 83.6 %shard_map.85 = bf16[320,1024]{1,0:T(8,128)(2,1)} custom-call(bf16[320,1024]{1,0:T(8,128)(2,1)} %bitcast.15, bf16[1024,7168]{1,0:T(8,128)(2,1)} %gate_hbm.1, bf16[1024,7168]{1,0:T(8,128)(2,1)} %up_hbm.1, bf16[7168,1024]{1,0:T(8,128)(2,1)} %down_hbm.1), custom_call_target="tpu_custom_call" | custom-call | flops 14092861440 | bytes 44040192 | tf_op jit(solution)/shard_map/pallas_call | solution.py:227
  113.2 3.6 %all-to-all-start.1 = ((bf16[8,40,1024]{2,1,0:T(8,128)(2,1)}), bf16[8,40,1024]{2,1,0:T(8,128)(2,1)S(1)}, u32[]{:S(2)}, u32[]{:S(2)}) async-start(bf16[8,40,1024]{2,1,0:T(8,128)(2,1)} %bitcast.14), calls=%async_computation.1 | async-start | bytes 1310720 | tf_op jit(solution)/shard_map/all_to_all | solution.py:287
  116.8 0.0 copy-done.1
  116.8 0.1 copy.26
  116.9 0.1 mul.37
  117.1 0.1 fusion.4
  117.2 26.5 %all-reduce = (f32[8]{0:T(128)S(1)}, f32[8]{0:T(128)S(1)}) all-reduce(f32[8]{0:T(128)S(1)} %convert_element_type.32, f32[8]{0:T(128)S(1)} %fusion.4), channel_id=1, replica_groups=mesh['ep'=8,'tp'=4] {'ep'}, use_global_device_ids=true, to_apply=%region_6.7 | all-reduce | flops 16 | bytes 128 | tf_op jit(solution)/shard_map/psum | solution.py:295
  143.7 0.0 copy-start.2
  143.7 0.6 multiply_reduce_fusion
  145.0 0.0 all-to-all-done.1
  145.0 1.3 convolution_convert_fusion.1
  146.3 0.0 copy-done.2
  (4 shorter events, 0.1 us)
Async XLA Ops:
  0.6 3.8 %copy-start = (bf16[128,1024]{1,0:T(8,128)(2,1)S(1)}, bf16[128,1024]{1,0:T(8,128)(2,1)}, u32[]{:S(2)}) copy-start(bf16[128,1024]{1,0:T(8,128)(2,1)} %param.6) | copy-start | bytes 786436
  29.6 87.2 %copy-start.1 = (f32[128,2]{0,1:T(2,128)S(1)}, f32[128,2]{0,1:T(2,128)}, u32[]{:S(2)}) copy-start(f32[128,2]{0,1:T(2,128)} %param.8) | copy-start | bytes 3076
  113.2 31.7 %all-to-all-start.1 = ((bf16[8,40,1024]{2,1,0:T(8,128)(2,1)}), bf16[8,40,1024]{2,1,0:T(8,128)(2,1)S(1)}, u32[]{:S(2)}, u32[]{:S(2)}) async-start(bf16[8,40,1024]{2,1,0:T(8,128)(2,1)} %bitcast.14), calls=%async_computation.1 | async-start | bytes 1310720 | tf_op jit(solution)/shard_map/all_to_all | solution.py:287
  143.7 2.6 %copy-start.2 = (f32[8]{0:T(128)}, f32[8]{0:T(128)S(1)}, u32[]{:S(2)}) copy-start(f32[8]{0:T(128)S(1)} %get-tuple-element.7) | copy-start | bytes 100

commit v2 on v1

--- a/solution.py
+++ b/solution.py
@@ -259,6 +259,68 @@
     )(received, gate_weight, up_weight, down_weight)
 
 
+def exchange_kernel(arrays, *refs):
+    sends, recvs, sems = refs[:arrays], refs[arrays:2 * arrays], refs[2 * arrays:]
+    send_sem, recv_sem, local_sem = sems
+    count = sends[0].shape[0]
+    me = lax.axis_index("ep")
+
+    def peer_of(k):
+        return lax.rem(me + k, count)
+
+    barrier = pltpu.get_barrier_semaphore()
+
+    def greet(k, carry):
+        pl.semaphore_signal(barrier, inc=1, device_id={"ep": peer_of(k)}, device_id_type=MESH)
+        return carry
+
+    def copy(a, k):
+        return pltpu.make_async_remote_copy(
+            src_ref=sends[a].at[peer_of(k)], dst_ref=recvs[a].at[me],
+            send_sem=send_sem.at[a, k], recv_sem=recv_sem.at[a, k],
+            device_id={"ep": peer_of(k)}, device_id_type=MESH,
+        )
+
+    def begin(k, carry):
+        for a in range(arrays):
+            copy(a, k).start()
+        return carry
+
+    def end(k, carry):
+        for a in range(arrays):
+            copy(a, k).wait()
+        return carry
+
+    lax.fori_loop(1, count, greet, 0)
+    stays = [
+        pltpu.make_async_copy(sends[a].at[me], recvs[a].at[me], local_sem.at[a])
+        for a in range(arrays)
+    ]
+    for stay in stays:
+        stay.start()
+    pl.semaphore_wait(barrier, count - 1)
+    lax.fori_loop(1, count, begin, 0)
+    lax.fori_loop(1, count, end, 0)
+    for stay in stays:
+        stay.wait()
+
+
+def exchange(blocks, number):
+    arrays, count = len(blocks), blocks[0].shape[0]
+    dma = pltpu.SemaphoreType.DMA
+    vmem = pl.BlockSpec(memory_space=pltpu.VMEM)
+    return pl.pallas_call(
+        functools.partial(exchange_kernel, arrays),
+        out_shape=[jax.ShapeDtypeStruct(b.shape, b.dtype) for b in blocks],
+        in_specs=[vmem] * arrays,
+        out_specs=[vmem] * arrays,
+        scratch_shapes=[dma((arrays, count)), dma((arrays, count)), dma((arrays,))],
+        compiler_params=pltpu.CompilerParams(
+            collective_id=number, has_side_effects=True, vmem_limit_bytes=60 * 1024 * 1024
+        ),
+    )(*blocks)
+
+
 def per_device(tokens, expert_ids, gates, gate_weight, up_weight, down_weight):
     count_tok = tokens.shape[0]
     quarter = tokens.shape[1]
@@ -280,19 +342,21 @@
     copies = jnp.broadcast_to(
         dispatched.reshape(EXPERTS, 1, CAP, quarter), (EXPERTS, replicas, CAP, quarter)
     )
-    received = lax.all_to_all(
-        copies.reshape(-1, quarter), "ep", split_axis=0, concat_axis=0, tiled=True
-    )
+    counts = jnp.sum(onehot, axis=0).astype(jnp.float32)
+    totals = jnp.sum(onehot.astype(jnp.float32) * gates.reshape(-1)[:, None], axis=0)
+    stats = jnp.pad(jnp.stack((counts, totals)), ((0, 6), (0, 128 - EXPERTS)))
+    stats = jnp.broadcast_to(stats[None], (lax.axis_size("ep"),) + stats.shape)
+    received, stats = exchange((copies.reshape(-1, CAP, quarter), stats), 1)
+    received = received.reshape(-1, quarter)
     partial_value = expert_rows(received, gate_weight, up_weight, down_weight)
-    returned = lax.all_to_all(partial_value, "ep", split_axis=0, concat_axis=0, tiled=True)
+    (returned,) = exchange((partial_value.reshape(-1, CAP, quarter),), 2)
     results = jnp.sum(returned.reshape(EXPERTS, replicas, CAP, quarter).astype(jnp.float32), axis=1)
     results = results.reshape(slots_all, quarter)
     mixed = jnp.dot(
         combine, results, precision=lax.Precision.HIGHEST, preferred_element_type=jnp.float32
     ).astype(jnp.bfloat16)
-    counts = jnp.sum(onehot, axis=0).astype(jnp.float32)
-    totals = jnp.sum(onehot.astype(jnp.float32) * gates.reshape(-1)[:, None], axis=0)
-    counts, totals = lax.psum((counts, totals), "ep")
+    stats = jnp.sum(stats, axis=0)
+    counts, totals = stats[0, :EXPERTS], stats[1, :EXPERTS]
     tokens_all = count_tok * lax.axis_size("ep")
     aux_loss = EXPERTS * jnp.sum(counts / (TOP * tokens_all) * (totals / tokens_all))
     return (mixed, counts, aux_loss)

time: 148 us -> 139 us (0.939); the launches traced: 147 us -> 137 us
  blocking collectives: 51.4 us -> 0 us
  Pallas kernels: 83.6 us -> 124 us
  starting transfers between devices: 3.55 us -> 0 us
  matrix products: 1.65 us -> 3.59 us
    pallas_call x0 -> x2, Pallas kernels: none -> 40.4 us  [exchange(): pl.pallas_call(functools.partial(exchange_kernel, arrays), out_shape=[jax...]
    psum x1 -> x0, blocking collectives: 26.5 us -> none  [per_device(): counts, totals = lax.psum((counts, totals), 'ep')]
    all_to_all x1 -> x0, blocking collectives: 24.9 us -> none  [per_device(): lax.all_to_all(copies.reshape(-1, quarter), 'ep', split_axis=0, concat_ax...]
    all_to_all x1 -> x0, starting transfers between devices: 3.55 us -> none  [per_device(): lax.all_to_all(partial_value, 'ep', split_axis=0, concat_axis=0, tiled=True)]
  transfers between devices with their start and end apart: 1 -> 0, of which waited for: 0 -> 0; matrix products, arithmetic and copies ran while one was open for 1% -> 0% of each run, Pallas kernels for 0% -> 0%
where the time goes in v2:
time: 139 us; the launch traced here: 137 us
  Pallas kernels  124 us (89%)
  matrix products  3.59 us (3%)
  other arithmetic  3.49 us (3%)
  local copies, waits for them, and re-layouts  3.08 us (2%)
  between operations  2.49 us (2%)
    pallas_call x1, Pallas kernels, expert_rows(): pl.pallas_call(functools.partial(expert_kernel, steps, chunk), out_shape=...  83.6 us
    pallas_call x2, Pallas kernels, exchange(): pl.pallas_call(functools.partial(exchange_kernel, arrays), out_shape=[jax...  40.4 us

profile of v2, /device:TPU:0, one launch (start us, length us, event | category | flops | bytes accessed | tf_op | source)
XLA Modules:
  0.0 136.6 jit_solution(6972822513029502399)
XLA Ops:
  0.6 0.0 copy-start
  0.6 0.8 copy.23
  1.5 0.1 eq.38
  1.6 0.1 eq.42
  1.8 0.6 reduce-window.6
  2.4 0.2 slice_reduce_fusion
  2.6 0.1 convert_reduce_fusion.1
  2.8 0.1 reduce_sum.70
  2.9 0.1 copy.25
  3.0 0.7 multiply_add_fusion
  3.7 0.8 copy.26
  4.5 0.1 mul.37
  4.6 0.1 fusion.4
  4.7 0.6 broadcast_in_dim.2.refs_1_
  5.4 0.8 convert_reduce_fusion
  6.1 0.0 copy-done
  6.1 1.2 convolution_convert_fusion
  7.3 19.3 %shard_map.85 = (bf16[8,40,1024]{2,1,0:T(8,128)(2,1)}, f32[8,8,128]{2,1,0:T(8,128)}) custom-call(bf16[8,40,1024]{2,1,0:T(8,128)(2,1)} %bitcast.22, f32[8,8,128]{2,1,0:T(8,128)} %broadcast_in_dim.2.refs_1_), custom_call_target="tpu_custom_call" | custom-call | tf_op jit(solution)/shard_map/pallas_call | solution.py:312
  26.6 0.0 copy-start.1
  26.6 83.6 %shard_map.86 = bf16[320,1024]{1,0:T(8,128)(2,1)} custom-call(bf16[320,1024]{1,0:T(8,128)(2,1)} %bitcast.26, bf16[1024,7168]{1,0:T(8,128)(2,1)} %gate_hbm.1, bf16[1024,7168]{1,0:T(8,128)(2,1)} %up_hbm.1, bf16[7168,1024]{1,0:T(8,128)(2,1)} %down_hbm.1), custom_call_target="tpu_custom_call" | custom-call | flops 14092861440 | bytes 44040192 | tf_op jit(solution)/shard_map/pallas_call | solution.py:227
  110.3 21.1 %shard_map.87 = bf16[8,40,1024]{2,1,0:T(8,128)(2,1)} custom-call(bf16[8,40,1024]{2,1,0:T(8,128)(2,1)} %bitcast.24), custom_call_target="tpu_custom_call" | custom-call | tf_op jit(solution)/shard_map/pallas_call | solution.py:312
  131.3 2.4 %convolution_convert_fusion.1 = bf16[128,1024]{1,0:T(8,128)(2,1)} fusion(f32[128,320]{0,1:T(8,128)S(1)} %get-tuple-element.10, bf16[320,1024]{1,0:T(8,128)(2,1)} %bitcast.23), kind=kOutput, calls=%fused_computation.1 | convolution fusion | flops 503447552 | bytes 1081344 | tf_op jit(solution)/shard_map/dot_general | solution.py:355
  133.7 0.0 copy-done.1
  133.8 1.1 fusion.6
  (6 shorter events, 0.1 us)
Async XLA Ops:
  0.6 5.5 %copy-start = (bf16[128,1024]{1,0:T(8,128)(2,1)S(1)}, bf16[128,1024]{1,0:T(8,128)(2,1)}, u32[]{:S(2)}) copy-start(bf16[128,1024]{1,0:T(8,128)(2,1)} %param.6) | copy-start | bytes 786436
  26.6 107.1 %copy-start.1 = (f32[8,8,128]{2,1,0:T(8,128)S(1)}, f32[8,8,128]{2,1,0:T(8,128)}, u32[]{:S(2)}) copy-start(f32[8,8,128]{2,1,0:T(8,128)} %get-tuple-element.6) | copy-start | bytes 98308
